TPU v7x, 128 devices: a whole 4x4x4 slice. The times are simulated.
128 devices in a mesh: dp: 64 (over z_hi, x, y, core), mp: 2 (over z_lo).
Axes of the slice: x: 4, y: 4, z: 4 (z_hi: 2, z_lo: 2; z = z_hi * 2 + z_lo), core: 2. Of those that a mesh axis runs over, the one named last changes fastest.
Arguments:
- inputs: bfloat16 [8192, 1792], P('dp', 'mp'), may hold values from -6 to 6
- cotangent: bfloat16 [8192, 1792], P('dp', 'mp'), may hold values from -6 to 6
- gate_weight: bfloat16 [9472, 1792], P(('mp', 'dp')), may hold values from -0.125 to 0.125
- up_weight: bfloat16 [9472, 1792], P(('mp', 'dp')), may hold values from -0.125 to 0.125
- down_weight: bfloat16 [9472, 1792], P(('mp', 'dp')), may hold values from -0.0625 to 0.0625
Outputs:
- input_grad: bfloat16 [8192, 1792], P('dp', 'mp')
- gate_grad: bfloat16 [9472, 1792], P(('mp', 'dp'))
All inputs are finite; a program needn't handle non-finite values.
Results may differ from a plain program's by a relative error of at most 0.009.
Values may be sent and summed in bfloat16 or wider, within the bound.
A program may use at most 320 MiB of HBM per device.

v0:
```python
import jax
import jax.numpy as jnp
from jax import lax
from jax.sharding import Mesh
from jax.sharding import PartitionSpec as P

DP = ("dp_0", "dp_1", "dp_2", "dp_3")
MP_DP = ("mp", "dp_0", "dp_1", "dp_2", "dp_3")


def side_by_side(arrays, axis, dim, along):
    widths = [a.shape[along] for a in arrays]
    both = jnp.concatenate(arrays, axis=along)
    filled = lax.all_gather(both, axis, axis=dim, tiled=True)
    return tuple(jnp.split(filled, [sum(widths[:k]) for k in range(1, len(widths))], axis=along))


def split_up(x, dim, peers):
    lengths = x.shape
    pieces = x.reshape(*lengths[:dim], peers, lengths[dim] // peers, *lengths[dim + 1 :])
    return jnp.moveaxis(pieces, dim, 0)


def sent_and_summed(x, axis, dim):
    peers = lax.axis_size(axis)
    pieces = lax.all_to_all(split_up(x, dim, peers), axis, 0, 0, tiled=True)
    return jnp.sum(pieces.astype(jnp.float32), axis=0)


def in_order(pieces, dim):
    pieces = jnp.moveaxis(pieces, 0, dim)
    lengths = pieces.shape
    return pieces.reshape(*lengths[:dim], lengths[dim] * lengths[dim + 1], *lengths[dim + 2 :])


def moved_by_axis(pieces, axes, turns):
    lengths = [lax.axis_size(a) for a in axes]
    pieces = pieces.reshape(*lengths, *pieces.shape[1:])
    for k in turns:
        pieces = lax.all_to_all(pieces, axes[k], split_axis=k, concat_axis=k, tiled=True)
    return pieces.reshape(-1, *pieces.shape[len(axes) :])


def exchange_by_chip(x, groups, turns, split_dim, concat_dim):
    peers = lax.axis_size(groups[0]) * lax.axis_size(groups[1])
    pieces = split_up(x, split_dim, peers)
    return in_order(moved_by_axis(pieces, groups, turns), concat_dim)


def tdot(left, right):
    return lax.dot_general(
        left, right, (((0,), (0,)), ((), ())), preferred_element_type=jnp.float32
    )


def rdot(left, right):
    return lax.dot_general(
        left, right, (((1,), (1,)), ((), ())), preferred_element_type=jnp.float32
    )


def per_device(inputs, cotangent, gate_weight, up_weight, down_weight):
    full_in, full_cot = side_by_side((inputs, cotangent), "mp", 1, 0)
    pieces = lax.all_gather((gate_weight, up_weight), DP, axis=0, tiled=True)
    stacked = jnp.stack([rdot(full_in, pieces[0]), rdot(full_in, pieces[1])])
    gate = stacked[0]
    up = stacked[1]
    dhidden = rdot(full_cot, lax.all_gather(down_weight, DP, axis=0, tiled=True))
    sig = jax.nn.sigmoid(gate)
    act = gate * sig
    dup = (dhidden * act).astype(jnp.bfloat16)
    dgate = (dhidden * up * sig * (1.0 + gate * (1.0 - sig))).astype(jnp.bfloat16)
    owned = exchange_by_chip(dgate, (("dp_0", "dp_1", "dp_2"), "dp_3"), (1, 0), 1, 0)
    gate_sum = tdot(owned, lax.all_gather(full_in, DP, axis=0, tiled=True))
    pieces = (
        lax.all_gather(gate_weight, DP, axis=0, tiled=True),
        lax.all_gather(up_weight, DP, axis=0, tiled=True),
    )
    total = jnp.dot(dgate, pieces[0], preferred_element_type=jnp.float32)
    partial_value = total + jnp.dot(dup, pieces[1], preferred_element_type=jnp.float32)
    input_grad = sent_and_summed(partial_value.astype(jnp.bfloat16), "mp", 1).astype(jnp.bfloat16)
    gate_grad = gate_sum.astype(jnp.bfloat16)
    return (input_grad, gate_grad)


def solution(mesh):
    torus = Mesh(
        mesh.devices.reshape(2, 4, 4, 2, mesh.shape["mp"]), ("dp_0", "dp_1", "dp_2", "dp_3", "mp")
    )
    return jax.shard_map(
        per_device,
        mesh=torus,
        in_specs=(P(DP, "mp"), P(DP, "mp"), P(MP_DP, None), P(MP_DP, None), P(MP_DP, None)),
        out_specs=(P(DP, "mp"), P(MP_DP, None)),
        check_vma=False,
    )
```

profile of v0, /device:TPU:1, one launch (start us, length us, event | category | flops | bytes accessed | tf_op | source)
XLA Modules:
  0.0 530.3 jit_solution(8056646707947620844)
XLA Ops:
  7.2 0.0 all-gather.10.cloned.1.call-start
  7.2 0.7 all-gather.10.cloned.1.call-update
  7.9 0.0 all-gather.12.cloned.1.call-start
  7.9 0.7 all-gather.12.cloned.1.call-update
  8.6 0.0 all-gather.14.cloned.1.call-start
  8.7 0.7 all-gather.14.cloned.1.call-update
  9.4 0.0 all-gather.8.cloned.1.call-start
  9.4 1.1 pad_maximum_fusion
  10.5 13.4 %all_gather.17 = bf16[256,1792]{1,0:T(8,128)(2,1)S(1)} all-gather(bf16[256,896]{1,0:T(8,128)(2,1)S(1)} %pad_maximum_fusion), channel_id=1, replica_groups=mesh['dp_0'=2,'dp_1'=4,'dp_2'=4,'dp_3'=2,'mp'=2] {'mp'}, dimensions={1}, use_global_device_ids=true | all-gather | bytes 1376256 | tf_op jit(solution)/shard_map/all_gather | solution.py:14
  23.9 0.8 split.9
  24.7 0.0 all-gather.8.cloned.1.call-update
  24.7 100.6 %all-gather.10.cloned.1.call-done = bf16[64,74,1792]{2,1,0:T(8,128)(2,1)} async-done(((bf16[1,74,1792]{2,1,0:T(8,128)(2,1)}), bf16[64,74,1792]{2,1,0:T(8,128)(2,1)}) %all-gather.10.cloned.1.call-update) | async-done | bytes 16973840 | tf_op jit(solution)/shard_map/all_gather | solution.py:68
  125.3 19.3 %reshape.17 = bf16[4736,1792]{1,0:T(8,128)(2,1)} reshape(bf16[64,74,1792]{2,1,0:T(8,128)(2,1)} %all-gather.10.cloned.1.call-done) | data formatting | bytes 33947648
  144.6 92.0 %all-gather.12.cloned.1.call-done = bf16[64,74,1792]{2,1,0:T(8,128)(2,1)} async-done(((bf16[1,74,1792]{2,1,0:T(8,128)(2,1)}), bf16[64,74,1792]{2,1,0:T(8,128)(2,1)}) %all-gather.12.cloned.1.call-update) | async-done | bytes 16973840 | tf_op jit(solution)/shard_map/all_gather | solution.py:64
  236.6 19.3 %reshape.19 = bf16[4736,1792]{1,0:T(8,128)(2,1)} reshape(bf16[64,74,1792]{2,1,0:T(8,128)(2,1)} %all-gather.12.cloned.1.call-done) | data formatting | bytes 33947648
  255.9 92.0 %all-gather.14.cloned.1.call-done = bf16[64,74,1792]{2,1,0:T(8,128)(2,1)} async-done(((bf16[1,74,1792]{2,1,0:T(8,128)(2,1)}), bf16[64,74,1792]{2,1,0:T(8,128)(2,1)}) %all-gather.14.cloned.1.call-update) | async-done | bytes 16973840 | tf_op jit(solution)/shard_map/all_gather | solution.py:64
  347.9 19.4 %reshape.21 = bf16[4736,1792]{1,0:T(8,128)(2,1)} reshape(bf16[64,74,1792]{2,1,0:T(8,128)(2,1)} %all-gather.14.cloned.1.call-done) | data formatting | bytes 33947648
  367.3 12.8 %fusion.5 = f32[128,4736]{1,0:T(8,128)} fusion(bf16[4736,1792]{1,0:T(8,128)(2,1)} %reshape.17, bf16[256,1792]{1,0:T(8,128)(2,1)S(1)} %all_gather.17), kind=kOutput, calls=%fused_computation.11 | convolution fusion | flops 2172649472 | bytes 19857408 | tf_op jit(solution)/shard_map/dot_general | solution.py:57
  380.0 13.2 %fusion.8 = f32[128,4736]{1,0:T(8,128)} fusion(bf16[4736,1792]{1,0:T(8,128)(2,1)} %reshape.21, bf16[256,1792]{1,0:T(8,128)(2,1)S(1)} %all_gather.17), kind=kOutput, calls=%fused_computation.15 | convolution fusion | flops 2172649472 | bytes 19857408 | tf_op jit(solution)/shard_map/dot_general | solution.py:57
  393.3 13.2 %fusion.2 = bf16[128,4736]{1,0:T(8,128)(2,1)S(1)} fusion(f32[128,4736]{1,0:T(8,128)} %fusion.5, bf16[4736,1792]{1,0:T(8,128)(2,1)} %reshape.19, f32[128,4736]{1,0:T(8,128)} %fusion.8, bf16[256,1792]{1,0:T(8,128)(2,1)S(1)} %all_gather.17), kind=kOutput, calls=%fused_computation.3 | convolution fusion | flops 2178711552 | bytes 23494656 | tf_op jit(solution)/shard_map/dot_general | solution.py:57
  406.4 1.5 copy.10
  407.9 0.0 copy-start
  407.9 0.0 copy-start.1
  407.9 8.4 %fusion.11 = f32[128,1792]{1,0:T(8,128)S(1)} fusion(bf16[128,4736]{1,0:T(8,128)(2,1)S(1)} %fusion.2, bf16[4736,1792]{1,0:T(8,128)(2,1)} %reshape.21), kind=kOutput, calls=%fused_computation.18 | convolution fusion | flops 2172649472 | bytes 19103744 | tf_op jit(solution)/shard_map/dot_general | solution.py:79
  416.4 0.0 copy-done
  416.4 0.0 copy-done.1
  416.4 9.6 %fusion.3 = bf16[128,1792]{1,0:T(8,128)(2,1)S(1)} fusion(f32[128,1792]{1,0:T(8,128)S(1)} %fusion.11, bf16[4736,1792]{1,0:T(8,128)(2,1)} %reshape.19, f32[128,4736]{1,0:T(8,128)S(1)} %copy-done, f32[128,4736]{1,0:T(8,128)S(1)} %copy-done.1), kind=kOutput, calls=%fused_computation.7 | convolution fusion | flops 2176745472 | bytes 23199744 | tf_op jit(solution)/shard_map/dot_general | solution.py:80
  426.0 0.8 copy.16
  426.8 0.3 reshape.14
  427.2 0.5 copy.11
  427.7 4.6 all_to_all.15
  432.2 3.5 all-to-all-start
  435.7 2.4 copy.12
  438.1 11.0 %all-to-all-done = bf16[2,128,896]{2,1,0:T(8,128)(2,1)S(1)} async-done(((bf16[2,128,896]{2,1,0:T(8,128)(2,1)}), bf16[2,128,896]{2,1,0:T(8,128)(2,1)S(1)}, u32[]{:S(2)}, u32[]{:S(2)}) %all-to-all-start) | async-done | bytes 458784 | tf_op jit(solution)/shard_map/all_to_all | solution.py:26
  449.0 7.4 %all-to-all-start.2 = ((bf16[32,2,128,74]{2,1,3,0:T(2,128)(2,1)}), bf16[32,2,128,74]{2,1,3,0:T(2,128)(2,1)S(1)}, u32[]{:S(2)}, u32[]{:S(2)}) async-start(bf16[32,2,128,74]{2,1,3,0:T(2,128)(2,1)} %copy.12), calls=%async_computation.2 | async-start | bytes 2424832 | tf_op jit(solution)/shard_map/all_to_all | solution.py:40
  456.4 0.8 reduce_sum.12
  457.2 17.5 %all-to-all-done.2 = bf16[32,2,128,74]{2,1,3,0:T(2,128)(2,1)S(1)} async-done(((bf16[32,2,128,74]{2,1,3,0:T(2,128)(2,1)}), bf16[32,2,128,74]{2,1,3,0:T(2,128)(2,1)S(1)}, u32[]{:S(2)}, u32[]{:S(2)}) %all-to-all-start.2) | async-done | bytes 1212448 | tf_op jit(solution)/shard_map/all_to_all | solution.py:40
  474.7 1.3 copy.13
  476.0 0.7 reshape_reshape.3
  476.8 34.3 %all-gather.8.cloned.1.call-done = bf16[8192,1792]{1,0:T(8,128)(2,1)} async-done(((bf16[128,1792]{1,0:T(8,128)(2,1)}), bf16[8192,1792]{1,0:T(8,128)(2,1)}) %all-gather.8.cloned.1.call-update) | async-done | bytes 29360144 | tf_op jit(solution)/shard_map/all_gather | solution.py:74
  511.1 12.7 %convolution_convert_fusion = bf16[74,1792]{1,0:T(8,128)(2,1)} fusion(bf16[8192,74]{0,1:T(8,128)(2,1)S(1)} %reshape_reshape.3, bf16[8192,1792]{1,0:T(8,128)(2,1)} %all-gather.8.cloned.1.call-done), kind=kOutput, calls=%fused_computation.8 | convolution fusion | flops 2172782080 | bytes 30837760 | tf_op jit(solution)/shard_map/dot_general | solution.py:51
Async XLA Ops:
  7.2 118.1 %all-gather.10.cloned.1.call-start = ((), (), s32[]{:S(2)}) async-start(), calls=%async_computation.4 | async-start | bytes 18636800 | tf_op jit(solution)/shard_map/all_gather | solution.py:68
  7.9 228.7 %all-gather.12.cloned.1.call-start = ((), (), s32[]{:S(2)}) async-start(), calls=%async_computation.5 | async-start | bytes 18636800 | tf_op jit(solution)/shard_map/all_gather | solution.py:64
  8.6 339.2 %all-gather.14.cloned.1.call-start = ((), (), s32[]{:S(2)}) async-start(), calls=%async_computation.6 | async-start | bytes 18636800 | tf_op jit(solution)/shard_map/all_gather | solution.py:64
  9.4 501.7 %all-gather.8.cloned.1.call-start = ((), (), s32[]{:S(2)}) async-start(), calls=%async_computation.3 | async-start | bytes 29818880 | tf_op jit(solution)/shard_map/all_gather | solution.py:74
  407.9 8.4 %copy-start = (f32[128,4736]{1,0:T(8,128)S(1)}, f32[128,4736]{1,0:T(8,128)}, u32[]{:S(2)}) copy-start(f32[128,4736]{1,0:T(8,128)} %fusion.5) | copy-start | bytes 7274500
  407.9 8.4 %copy-start.1 = (f32[128,4736]{1,0:T(8,128)S(1)}, f32[128,4736]{1,0:T(8,128)}, u32[]{:S(2)}) copy-start(f32[128,4736]{1,0:T(8,128)} %fusion.8) | copy-start | bytes 7274500
  432.2 16.8 %all-to-all-start = ((bf16[2,128,896]{2,1,0:T(8,128)(2,1)}), bf16[2,128,896]{2,1,0:T(8,128)(2,1)S(1)}, u32[]{:S(2)}, u32[]{:S(2)}) async-start(bf16[2,128,896]{2,1,0:T(8,128)(2,1)} %bitcast.24), calls=%async_computation | async-start | bytes 917504 | tf_op jit(solution)/shard_map/all_to_all | solution.py:26
  449.0 25.7 %all-to-all-start.2 = ((bf16[32,2,128,74]{2,1,3,0:T(2,128)(2,1)}), bf16[32,2,128,74]{2,1,3,0:T(2,128)(2,1)S(1)}, u32[]{:S(2)}, u32[]{:S(2)}) async-start(bf16[32,2,128,74]{2,1,3,0:T(2,128)(2,1)} %copy.12), calls=%async_computation.2 | async-start | bytes 2424832 | tf_op jit(solution)/shard_map/all_to_all | solution.py:40
Sparse Core Ops, SparseCore 0:
  11.1 114.1 all-gather.9
  128.4 108.1 all-gather.11
  239.7 108.1 all-gather.13
  350.9 160.2 all-gather.7
where the time goes:
time: 532 us; the launch traced here: 530 us
  waiting for transfers between devices  349 us (66%)
  matrix products  69.9 us (13%)
  local copies, waits for them, and re-layouts  66.4 us (12%)
  blocking collectives  17.9 us (3%)
  between operations  13.9 us (3%)
  starting transfers between devices  11 us (2%)
    all_gather x2, waiting for transfers between devices, per_device(): pieces = lax.all_gather((gate_weight, up_weight), DP, axis=0, tiled=True)  184 us
    all_gather x1, waiting for transfers between devices, per_device(): lax.all_gather(down_weight, DP, axis=0, tiled=True)  101 us
    unnamed x7, local copies, waits for them, and re-layouts  58 us
    dot_general x3, matrix products, rdot(): lax.dot_general(left, right, (((1,), (1,)), ((), ())), preferred_element_...  39.2 us
    all_gather x1, waiting for transfers between devices, per_device(): gate_sum = tdot(owned, lax.all_gather(full_in, DP, axis=0, tiled=True))  34.3 us
    all_to_all x1, waiting for transfers between devices, moved_by_axis(): lax.all_to_all(pieces, axes[k], split_axis=k, concat_axis=k, tiled=True)  17.5 us
    all_gather x1, blocking collectives, side_by_side(): filled = lax.all_gather(both, axis, axis=dim, tiled=True)  13.4 us
    dot_general x1, matrix products, tdot(): lax.dot_general(left, right, (((0,), (0,)), ((), ())), preferred_element_...  12.7 us
  transfers between devices with their start and end apart: 6, of which 6 were waited for; matrix products, arithmetic and copies ran while one was open for 24% of the time, Pallas kernels for 0%

commit v1 on v0

--- a/solution.py
+++ b/solution.py
@@ -65,7 +65,12 @@
     stacked = jnp.stack([rdot(full_in, pieces[0]), rdot(full_in, pieces[1])])
     gate = stacked[0]
     up = stacked[1]
-    dhidden = rdot(full_cot, lax.all_gather(down_weight, DP, axis=0, tiled=True))
+    dhidden = rdot(
+        full_cot,
+        jnp.concatenate(
+            lax.all_to_all(jnp.stack([down_weight] * lax.axis_size(DP)), DP, 0, 0), axis=0
+        ),
+    )
     sig = jax.nn.sigmoid(gate)
     act = gate * sig
     dup = (dhidden * act).astype(jnp.bfloat16)

time: 532 us -> 604 us (1.14)
  blocking collectives: 17.9 us -> 247 us
  waiting for transfers between devices: 349 us -> 193 us
    all_to_all x0 -> x1, blocking collectives: none -> 229 us  [per_device(): lax.all_to_all(jnp.stack([down_weight] * lax.axis_size(DP)), DP, 0, 0)]
    all_gather x1 -> x0, waiting for transfers between devices: 101 us -> none  [per_device(): lax.all_gather(down_weight, DP, axis=0, tiled=True)]
    all_gather x2, waiting for transfers between devices: 184 us -> 114 us  [per_device(): pieces = lax.all_gather((gate_weight, up_weight), DP, axis=0, tiled=True)]
    reshape x0 -> x1, local copies, waits for them, and re-layouts: none -> 19.5 us  [per_device(): jnp.concatenate(lax.all_to_all(jnp.stack([down_weight] * lax.axis_size(DP...]
    unnamed x7 -> x8, local copies, waits for them, and re-layouts: 58 us -> 38.7 us
    all_gather x1, waiting for transfers between devices: 34.3 us -> 50.4 us  [per_device(): gate_sum = tdot(owned, lax.all_gather(full_in, DP, axis=0, tiled=True))]
  transfers between devices with their start and end apart: 6 -> 5, of which waited for: 6 -> 5; matrix products, arithmetic and copies ran while one was open for 24% -> 21% of each run, Pallas kernels for 0% -> 0%
where the time goes in v1:
time: 604 us; the launch traced here: 602 us
  blocking collectives  247 us (41%)
  waiting for transfers between devices  193 us (32%)
  matrix products  69.1 us (11%)
  local copies, waits for them, and re-layouts  68 us (11%)
  between operations  13.9 us (2%)
  starting transfers between devices  8.61 us (1%)
    all_to_all x1, blocking collectives, per_device(): lax.all_to_all(jnp.stack([down_weight] * lax.axis_size(DP)), DP, 0, 0)  229 us
    all_gather x2, waiting for transfers between devices, per_device(): pieces = lax.all_gather((gate_weight, up_weight), DP, axis=0, tiled=True)  114 us
    all_gather x1, waiting for transfers between devices, per_device(): gate_sum = tdot(owned, lax.all_gather(full_in, DP, axis=0, tiled=True))  50.4 us
    dot_general x3, matrix products, rdot(): lax.dot_general(left, right, (((1,), (1,)), ((), ())), preferred_element_...  39.1 us
    unnamed x8, local copies, waits for them, and re-layouts  38.7 us
    reshape x1, local copies, waits for them, and re-layouts, per_device(): jnp.concatenate(lax.all_to_all(jnp.stack([down_weight] * lax.axis_size(DP...  19.5 us
    all_to_all x1, waiting for transfers between devices, moved_by_axis(): lax.all_to_all(pieces, axes[k], split_axis=k, concat_axis=k, tiled=True)  17.5 us
    all_gather x1, blocking collectives, side_by_side(): filled = lax.all_gather(both, axis, axis=dim, tiled=True)  13.4 us
  transfers between devices with their start and end apart: 5, of which 5 were waited for; matrix products, arithmetic and copies ran while one was open for 21% of the time, Pallas kernels for 0%

profile of v1, /device:TPU:1, one launch (start us, length us, event | category | flops | bytes accessed | tf_op | source)
XLA Modules:
  0.0 602.3 jit_solution(5598862981649085335)
XLA Ops:
  7.2 0.0 copy-start.2
  7.2 0.0 all-gather.8.cloned.1.call-start
  7.2 0.7 all-gather.8.cloned.1.call-update
  7.9 0.0 all-gather.10.cloned.1.call-start
  8.0 0.7 all-gather.10.cloned.1.call-update
  8.7 0.0 all-gather.6.cloned.1.call-start
  8.7 1.1 pad_maximum_fusion
  9.8 13.4 %all_gather.14 = bf16[256,1792]{1,0:T(8,128)(2,1)S(1)} all-gather(bf16[256,896]{1,0:T(8,128)(2,1)S(1)} %pad_maximum_fusion), channel_id=1, replica_groups=mesh['dp_0'=2,'dp_1'=4,'dp_2'=4,'dp_3'=2,'mp'=2] {'mp'}, dimensions={1}, use_global_device_ids=true | all-gather | bytes 1376256 | tf_op jit(solution)/shard_map/all_gather | solution.py:14
  23.2 0.8 split.9
  24.0 0.0 all-gather.6.cloned.1.call-update
  24.0 0.0 copy-done.2
  24.0 1.6 stack.2
  25.6 228.7 %all_to_all.20 = bf16[64,74,1792]{2,1,0:T(8,128)(2,1)} all-to-all(bf16[64,74,1792]{2,1,0:T(8,128)(2,1)S(1)} %stack.2), channel_id=1, replica_groups=mesh['dp_0'=2,'dp_1'=4,'dp_2'=4,'dp_3'=2,'mp'=2] {'dp_0','dp_1','dp_2','..., dimensions={0} | all-to-all | bytes 33947648 | tf_op jit(solution)/shard_map/all_to_all | solution.py:71
  254.2 19.5 %reshape.18 = bf16[4736,1792]{1,0:T(8,128)(2,1)} reshape(bf16[64,74,1792]{2,1,0:T(8,128)(2,1)} %all_to_all.20) | data formatting | bytes 33947648 | tf_op jit(solution)/shard_map/reshape | solution.py:70
  273.7 13.0 %fusion.5 = f32[128,4736]{1,0:T(8,128)} fusion(bf16[4736,1792]{1,0:T(8,128)(2,1)} %reshape.18, bf16[256,1792]{1,0:T(8,128)(2,1)S(1)} %all_gather.14), kind=kOutput, calls=%fused_computation.11 | convolution fusion | flops 2172649472 | bytes 19857408 | tf_op jit(solution)/shard_map/dot_general | solution.py:57
  286.7 21.1 %all-gather.8.cloned.1.call-done = bf16[64,74,1792]{2,1,0:T(8,128)(2,1)} async-done(((bf16[1,74,1792]{2,1,0:T(8,128)(2,1)}), bf16[64,74,1792]{2,1,0:T(8,128)(2,1)}) %all-gather.8.cloned.1.call-update) | async-done | bytes 16973840 | tf_op jit(solution)/shard_map/all_gather | solution.py:64
  307.7 19.3 %reshape.23 = bf16[4736,1792]{1,0:T(8,128)(2,1)} reshape(bf16[64,74,1792]{2,1,0:T(8,128)(2,1)} %all-gather.8.cloned.1.call-done) | data formatting | bytes 33947648
  327.1 92.6 %all-gather.10.cloned.1.call-done = bf16[64,74,1792]{2,1,0:T(8,128)(2,1)} async-done(((bf16[1,74,1792]{2,1,0:T(8,128)(2,1)}), bf16[64,74,1792]{2,1,0:T(8,128)(2,1)}) %all-gather.10.cloned.1.call-update) | async-done | bytes 16973840 | tf_op jit(solution)/shard_map/all_gather | solution.py:64
  419.7 19.3 %reshape.25 = bf16[4736,1792]{1,0:T(8,128)(2,1)} reshape(bf16[64,74,1792]{2,1,0:T(8,128)(2,1)} %all-gather.10.cloned.1.call-done) | data formatting | bytes 33947648
  439.0 12.8 %fusion.8 = f32[128,4736]{1,0:T(8,128)} fusion(bf16[4736,1792]{1,0:T(8,128)(2,1)} %reshape.25, bf16[256,1792]{1,0:T(8,128)(2,1)S(1)} %all_gather.14), kind=kOutput, calls=%fused_computation.15 | convolution fusion | flops 2172649472 | bytes 19857408 | tf_op jit(solution)/shard_map/dot_general | solution.py:57
  451.8 13.3 %fusion.2 = bf16[128,4736]{1,0:T(8,128)(2,1)S(1)} fusion(f32[128,4736]{1,0:T(8,128)} %fusion.5, bf16[4736,1792]{1,0:T(8,128)(2,1)} %reshape.23, f32[128,4736]{1,0:T(8,128)} %fusion.8, bf16[256,1792]{1,0:T(8,128)(2,1)S(1)} %all_gather.14), kind=kOutput, calls=%fused_computation.3 | convolution fusion | flops 2178711552 | bytes 23494656 | tf_op jit(solution)/shard_map/dot_general | solution.py:57
  465.1 1.5 copy.10
  466.6 0.0 copy-start
  466.6 0.0 copy-start.1
  466.6 8.8 %fusion.11 = f32[128,1792]{1,0:T(8,128)S(1)} fusion(bf16[128,4736]{1,0:T(8,128)(2,1)S(1)} %fusion.2, bf16[4736,1792]{1,0:T(8,128)(2,1)} %reshape.25), kind=kOutput, calls=%fused_computation.18 | convolution fusion | flops 2172649472 | bytes 19103744 | tf_op jit(solution)/shard_map/dot_general | solution.py:84
  475.4 0.0 copy-done
  475.4 0.0 copy-done.1
  475.5 8.6 %fusion.3 = bf16[128,1792]{1,0:T(8,128)(2,1)S(1)} fusion(f32[128,1792]{1,0:T(8,128)S(1)} %fusion.11, bf16[4736,1792]{1,0:T(8,128)(2,1)} %reshape.23, f32[128,4736]{1,0:T(8,128)S(1)} %copy-done, f32[128,4736]{1,0:T(8,128)S(1)} %copy-done.1), kind=kOutput, calls=%fused_computation.7 | convolution fusion | flops 2176745472 | bytes 23199744 | tf_op jit(solution)/shard_map/dot_general | solution.py:85
  484.0 0.8 copy.16
  484.8 0.3 reshape.20
  485.2 0.5 copy.11
  485.7 5.4 all_to_all.21
  491.1 3.5 all-to-all-start.1
  494.6 2.3 copy.12
  496.8 10.4 %all-to-all-done.1 = bf16[2,128,896]{2,1,0:T(8,128)(2,1)S(1)} async-done(((bf16[2,128,896]{2,1,0:T(8,128)(2,1)}), bf16[2,128,896]{2,1,0:T(8,128)(2,1)S(1)}, u32[]{:S(2)}, u32[]{:S(2)}) %all-to-all-start.1) | async-done | bytes 458784 | tf_op jit(solution)/shard_map/all_to_all | solution.py:26
  507.3 5.0 all-to-all-start.3
  512.3 0.8 reduce_sum.12
  513.1 17.5 %all-to-all-done.3 = bf16[32,2,128,74]{2,1,3,0:T(2,128)(2,1)S(1)} async-done(((bf16[32,2,128,74]{2,1,3,0:T(2,128)(2,1)}), bf16[32,2,128,74]{2,1,3,0:T(2,128)(2,1)S(1)}, u32[]{:S(2)}, u32[]{:S(2)}) %all-to-all-start.3) | async-done | bytes 1212448 | tf_op jit(solution)/shard_map/all_to_all | solution.py:40
  530.6 1.3 copy.13
  531.9 0.7 reshape_reshape.3
  532.7 50.4 %all-gather.6.cloned.1.call-done = bf16[8192,1792]{1,0:T(8,128)(2,1)} async-done(((bf16[128,1792]{1,0:T(8,128)(2,1)}), bf16[8192,1792]{1,0:T(8,128)(2,1)}) %all-gather.6.cloned.1.call-update) | async-done | bytes 29360144 | tf_op jit(solution)/shard_map/all_gather | solution.py:79
  583.0 12.7 %convolution_convert_fusion = bf16[74,1792]{1,0:T(8,128)(2,1)} fusion(bf16[8192,74]{0,1:T(8,128)(2,1)S(1)} %reshape_reshape.3, bf16[8192,1792]{1,0:T(8,128)(2,1)} %all-gather.6.cloned.1.call-done), kind=kOutput, calls=%fused_computation.8 | convolution fusion | flops 2172782080 | bytes 30837760 | tf_op jit(solution)/shard_map/dot_general | solution.py:51
Async XLA Ops:
  7.2 16.8 %copy-start.2 = (bf16[74,1792]{1,0:T(8,128)(2,1)S(1)}, bf16[74,1792]{1,0:T(8,128)(2,1)}, u32[]{:S(2)}) copy-start(bf16[74,1792]{1,0:T(8,128)(2,1)} %param.9) | copy-start | bytes 795652
  7.2 300.6 %all-gather.8.cloned.1.call-start = ((), (), s32[]{:S(2)}) async-start(), calls=%async_computation.5 | async-start | bytes 18636800 | tf_op jit(solution)/shard_map/all_gather | solution.py:64
  7.9 411.8 %all-gather.10.cloned.1.call-start = ((), (), s32[]{:S(2)}) async-start(), calls=%async_computation.6 | async-start | bytes 18636800 | tf_op jit(solution)/shard_map/all_gather | solution.py:64
  8.7 574.4 %all-gather.6.cloned.1.call-start = ((), (), s32[]{:S(2)}) async-start(), calls=%async_computation.4 | async-start | bytes 29818880 | tf_op jit(solution)/shard_map/all_gather | solution.py:79
  466.6 8.8 %copy-start = (f32[128,4736]{1,0:T(8,128)S(1)}, f32[128,4736]{1,0:T(8,128)}, u32[]{:S(2)}) copy-start(f32[128,4736]{1,0:T(8,128)} %fusion.5) | copy-start | bytes 7274500
  466.6 8.8 %copy-start.1 = (f32[128,4736]{1,0:T(8,128)S(1)}, f32[128,4736]{1,0:T(8,128)}, u32[]{:S(2)}) copy-start(f32[128,4736]{1,0:T(8,128)} %fusion.8) | copy-start | bytes 7274500
  491.1 16.2 %all-to-all-start.1 = ((bf16[2,128,896]{2,1,0:T(8,128)(2,1)}), bf16[2,128,896]{2,1,0:T(8,128)(2,1)S(1)}, u32[]{:S(2)}, u32[]{:S(2)}) async-start(bf16[2,128,896]{2,1,0:T(8,128)(2,1)} %bitcast.23), calls=%async_computation.1 | async-start | bytes 917504 | tf_op jit(solution)/shard_map/all_to_all | solution.py:26
  507.3 23.3 %all-to-all-start.3 = ((bf16[32,2,128,74]{2,1,3,0:T(2,128)(2,1)}), bf16[32,2,128,74]{2,1,3,0:T(2,128)(2,1)S(1)}, u32[]{:S(2)}, u32[]{:S(2)}) async-start(bf16[32,2,128,74]{2,1,3,0:T(2,128)(2,1)} %copy.12), calls=%async_computation.3 | async-start | bytes 2424832 | tf_op jit(solution)/shard_map/all_to_all | solution.py:40
Sparse Core Ops, SparseCore 0:
  11.1 296.6 all-gather.7
  310.9 108.7 all-gather.9
  422.8 160.2 all-gather.5
